TPU v7x, 512 devices: a whole 4x8x8 slice. The times are simulated.
512 devices in a mesh: tok: 64 (over y, x, core), ch: 8 (over z).
Axes of the slice: x: 4, y: 8, z: 8, core: 2. Of those that a mesh axis runs over, the one named last changes fastest.
Arguments:
- fields: float32 [16384, 1024], P('tok', 'ch'), may hold values from -20 to 20
- gain_one: float32 [1024], P('ch'), may hold values from 0.1 to 1.9
- tok_in_weight: float32 [3072, 16384], P('ch', 'tok'), may hold values from -0.046875 to 0.046875
- tok_in_bias: float32 [3072], P('ch'), may hold values from -3 to 3
- tok_out_weight: float32 [16384, 3072], P('tok', 'ch'), may hold values from -0.109375 to 0.109375
- gain_two: float32 [1024], P('ch'), may hold values from 0.1 to 1.9
- ch_in_weight: float32 [1024, 6144], P('tok', 'ch'), may hold values from -0.1875 to 0.1875
- ch_in_bias: float32 [6144], P('ch'), may hold values from -3 to 3
- ch_out_weight: float32 [6144, 1024], P('ch', 'tok'), may hold values from -0.078125 to 0.078125
Outputs:
- block_out: float32 [16384, 1024], P('tok', 'ch')
All inputs are finite; a program needn't handle non-finite values.
Results may differ from a plain program's by a relative error of at most 0.000086.
Values sent between devices are 32-bit elements; how exact they have to be, the bound alone decides.
A program may use at most 64 MiB of HBM per device.

v0:
```python
import jax
import jax.numpy as jnp
from jax import lax
from jax.sharding import PartitionSpec as P

epsilon = 1e-05
highest = lax.Precision.HIGHEST


def matmul(left, right):
    return jnp.dot(left, right, precision=highest, preferred_element_type=jnp.float32)


def shards(
    fields,
    gain_one,
    tok_in_weight,
    tok_in_bias,
    tok_out_weight,
    gain_two,
    ch_in_weight,
    ch_in_bias,
    ch_out_weight,
):
    tok_rows, ch_width = fields.shape
    channels = ch_width * lax.axis_size("ch")
    row_total = lax.psum(jnp.sum(fields, axis=1, keepdims=True), "ch")
    centred = fields - row_total / channels
    row_spread = lax.psum(jnp.sum(centred * centred, axis=1, keepdims=True), "ch")
    normed_part = centred * lax.rsqrt(row_spread / channels + epsilon) * gain_one
    normed = lax.all_gather(normed_part, "ch", axis=1, tiled=True)
    columns = normed
    summed_cols = lax.psum_scatter(
        lax.dot_general(
            columns,
            tok_in_weight,
            (((0,), (1,)), ((), ())),
            precision=highest,
            preferred_element_type=jnp.float32,
        ),
        "tok",
        scatter_dimension=0,
        tiled=True,
    )
    activated = jax.nn.gelu(summed_cols + tok_in_bias[None, :], approximate=False)
    partial_value = lax.dot_general(
        tok_out_weight,
        lax.all_gather(activated, "tok", axis=0, tiled=True),
        (((1,), (1,)), ((), ())),
        precision=highest,
        preferred_element_type=jnp.float32,
    )
    mixed_sum = lax.psum_scatter(partial_value, "ch", scatter_dimension=1, tiled=True)
    kept_rows = fields + mixed_sum
    row_total_two = lax.psum(jnp.sum(kept_rows, axis=1, keepdims=True), "ch")
    centred_two = kept_rows - row_total_two / channels
    row_spread_two = lax.psum(jnp.sum(centred_two * centred_two, axis=1, keepdims=True), "ch")
    normed_part_two = centred_two * lax.rsqrt(row_spread_two / channels + epsilon) * gain_two
    normed_two = lax.all_gather(normed_part_two, "ch", axis=1, tiled=True)
    columns = normed_two
    hidden_sum = matmul(columns, lax.all_gather(ch_in_weight, "tok", axis=0, tiled=True))
    activated_two = jax.nn.gelu(hidden_sum + ch_in_bias[None, :], approximate=False)
    channel_terms = matmul(activated_two, lax.all_gather(ch_out_weight, "tok", axis=1, tiled=True))
    return kept_rows + lax.psum_scatter(channel_terms, "ch", scatter_dimension=1, tiled=True)


def solution(mesh):
    in_specs = (
        P("tok", "ch"),
        P("ch"),
        P("ch", "tok"),
        P("ch"),
        P("tok", "ch"),
        P("ch"),
        P("tok", "ch"),
        P("ch"),
        P("ch", "tok"),
    )
    out_specs = P("tok", "ch")
    return jax.shard_map(shards, mesh=mesh, in_specs=in_specs, out_specs=out_specs, check_vma=False)
```

profile of v0, /device:TPU:2, one launch (start us, length us, event | category | flops | bytes accessed | tf_op | source)
XLA Modules:
  0.0 690.1 jit_solution(6796700619415421560)
XLA Ops:
  6.5 0.0 copy-start
  6.5 0.0 copy-start.4
  6.5 0.0 copy-start.2
  6.5 0.0 all-gather.6.cloned.1.call-start
  6.5 1.1 reduce_sum.36
  7.6 23.2 %psum.28 = f32[256,1]{0,1:T(1,128)S(1)} all-reduce(f32[256,1]{0,1:T(1,128)S(1)} %bitcast.25), channel_id=1, replica_groups=mesh['tok'=64,'ch'=8] {'ch'}, use_global_device_ids=true, to_apply=%region_1.0 | all-reduce | flops 256 | bytes 2048 | tf_op jit(solution)/shard_map/psum | solution.py:27
  30.8 1.1 multiply_reduce_fusion.1
  31.9 14.2 %psum.29 = f32[256,1]{0,1:T(1,128)S(1)} all-reduce(f32[256,1]{0,1:T(1,128)S(1)} %bitcast.26), channel_id=1, replica_groups=mesh['tok'=64,'ch'=8] {'ch'}, use_global_device_ids=true, to_apply=%region_3.0 | all-reduce | flops 256 | bytes 2048 | tf_op jit(solution)/shard_map/psum | solution.py:29
  46.1 1.7 multiply_multiply_fusion.6
  47.8 0.0 all-gather.6.cloned.1.call-update
  47.8 0.0 all-reduce.3.cloned.1.call-start
  47.9 40.3 %all-gather.6.cloned.1.call-done = f32[256,1024]{1,0:T(8,128)} async-done(((f32[256,128]{1,0:T(8,128)}), f32[256,1024]{1,0:T(8,128)}) %all-gather.6.cloned.1.call-update) | async-done | bytes 1048592 | tf_op jit(solution)/shard_map/all_gather | solution.py:31
  88.2 0.0 copy-done
  88.2 5.8 fusion.129
  94.0 0.0 copy-start.1
  94.0 0.0 copy-start.5
  94.0 0.0 copy-start.3
  94.0 0.0 all-reduce.3.cloned.1.call-update
  94.0 0.0 all-gather.8.cloned.1.call-start
  94.1 1.3 dynamic-slice
  96.0 197.0 %all-reduce.3.cloned.1.call-done = f32[1024,384]{1,0:T(8,128)} async-done(((f32[1024,384]{1,0:T(8,128)}), f32[1024,384]{1,0:T(8,128)}) %all-reduce.3.cloned.1.call-update) | async-done | bytes 1572880
  293.0 0.0 copy-done.4
  293.0 1.4 fusion.90
  294.4 0.0 all-gather.8.cloned.1.call-update
  294.4 0.0 reduce-scatter.3.cloned.1.call-start
  294.5 82.7 %all-gather.8.cloned.1.call-done = f32[1024,384]{1,0:T(8,128)} async-done(((f32[16,384]{1,0:T(8,128)}), f32[1024,384]{1,0:T(8,128)}) %all-gather.8.cloned.1.call-update) | async-done | bytes 1572880 | tf_op jit(solution)/shard_map/all_gather | solution.py:48
  377.1 0.0 copy-done.2
  377.2 4.2 convolution_bitcast_fusion
  381.3 0.0 reduce-scatter.3.cloned.1.call-update
  381.4 0.0 all-gather.12.cloned.1.call-start
  381.4 0.5 all-gather.12.cloned.1.call-update
  382.0 0.0 all-gather.10.cloned.1.call-start
  382.0 0.0 copy-done.1
  382.0 0.1 copy.16
  382.1 40.9 %reduce-scatter.3.cloned.1.call-done = f32[256,128]{0,1:T(8,128)} async-done(((f32[256,1024]{0,1:T(8,128)}), f32[256,128]{0,1:T(8,128)}) %reduce-scatter.3.cloned.1.call-update) | async-done | bytes 131088 | tf_op jit(solution)/shard_map/reduce_scatter | solution.py:53
  423.0 0.9 fusion.128
  424.0 15.4 %psum.30 = f32[256,1]{0,1:T(1,128)S(1)} all-reduce(f32[256,1]{0,1:T(1,128)S(1)} %bitcast.22), channel_id=1, replica_groups=mesh['tok'=64,'ch'=8] {'ch'}, use_global_device_ids=true, to_apply=%region_7.0 | all-reduce | flops 256 | bytes 2048 | tf_op jit(solution)/shard_map/psum | solution.py:55
  439.4 14.9 %psum.31 = f32[256,1]{0,1:T(1,128)S(1)} all-reduce(f32[256,1]{0,1:T(1,128)S(1)} %bitcast.27), channel_id=1, replica_groups=mesh['tok'=64,'ch'=8] {'ch'}, use_global_device_ids=true, to_apply=%region_9.0 | all-reduce | flops 256 | bytes 2048 | tf_op jit(solution)/shard_map/psum | solution.py:57
  454.3 0.0 copy-done.5
  454.3 0.7 multiply_multiply_fusion.5
  455.1 0.0 all-gather.10.cloned.1.call-update
  455.1 0.0 all-gather.14.cloned.1.call-start
  455.2 0.7 all-gather.14.cloned.1.call-update
  455.9 0.2 reduce-scatter.5.cloned.1.call-start
  456.1 50.2 %all-gather.12.cloned.1.call-done = f32[1024,768]{1,0:T(8,128)} async-done(((f32[16,768]{1,0:T(8,128)}), f32[1024,768]{1,0:T(8,128)}) %all-gather.12.cloned.1.call-update) | async-done | bytes 3145744 | tf_op jit(solution)/shard_map/all_gather | solution.py:61
  506.3 42.9 %all-gather.10.cloned.1.call-done = f32[256,1024]{0,1:T(8,128)} async-done(((f32[256,128]{0,1:T(8,128)}), f32[256,1024]{0,1:T(8,128)}) %all-gather.10.cloned.1.call-update) | async-done | bytes 1048592 | tf_op jit(solution)/shard_map/all_gather | solution.py:59
  549.2 0.0 copy-done.3
  549.2 5.0 convolution_add_fusion
  554.2 78.4 %all-gather.14.cloned.1.call-done = f32[768,1024]{0,1:T(8,128)} async-done(((f32[768,16]{0,1:T(8,128)}), f32[768,1024]{0,1:T(8,128)}) %all-gather.14.cloned.1.call-update) | async-done | bytes 3145744 | tf_op jit(solution)/shard_map/all_gather | solution.py:63
  632.7 7.3 %fusion.2 = f32[256,1024]{0,1:T(8,128)} fusion(f32[768,1024]{0,1:T(8,128)} %all-gather.14.cloned.1.call-done, f32[256,768]{1,0:T(8,128)S(1)} %convolution_add_fusion), kind=kOutput, calls=%fused_computation.5 | convolution fusion | flops 2428502016 | bytes 4980736 | tf_op jit(solution)/shard_map/dot_general | solution.py:11
  640.0 0.0 reduce-scatter.5.cloned.1.call-update
  640.0 41.6 %reduce-scatter.5.cloned.1.call-done = f32[256,128]{0,1:T(8,128)} async-done(((f32[256,1024]{0,1:T(8,128)}), f32[256,128]{0,1:T(8,128)}) %reduce-scatter.5.cloned.1.call-update) | async-done | bytes 131088 | tf_op jit(solution)/shard_map/reduce_scatter | solution.py:64
  681.6 0.9 add.49
  682.5 0.8 copy.18
  (5 shorter events, 0.1 us)
Async XLA Ops:
  6.5 81.7 %copy-start = (f32[384,256]{1,0:T(8,128)S(1)}, f32[384,256]{1,0:T(8,128)}, u32[]{:S(2)}) copy-start(f32[384,256]{1,0:T(8,128)} %param.11) | copy-start | bytes 1179652
  6.5 286.4 %copy-start.4 = (f32[384]{0:T(512)S(1)}, f32[384]{0:T(512)}, u32[]{:S(2)}) copy-start(f32[384]{0:T(512)} %param.12) | copy-start | bytes 4612
  6.5 370.6 %copy-start.2 = (f32[256,384]{1,0:T(8,128)S(1)}, f32[256,384]{1,0:T(8,128)}, u32[]{:S(2)}) copy-start(f32[256,384]{1,0:T(8,128)} %param.13) | copy-start | bytes 1179652
  6.5 81.6 %all-gather.6.cloned.1.call-start = ((), (), s32[]{:S(2)}) async-start(), calls=%async_computation.2 | async-start | bytes 1179648 | tf_op jit(solution)/shard_map/all_gather | solution.py:31
  47.8 245.2 %all-reduce.3.cloned.1.call-start = ((), (), s32[]{:S(2)}) async-start(), calls=%async_computation.9 | async-start | bytes 3145728
  94.0 288.0 %copy-start.1 = (f32[256,128]{1,0:T(8,128)S(1)}, f32[256,128]{1,0:T(8,128)}, u32[]{:S(2)}) copy-start(f32[256,128]{1,0:T(8,128)} %param.9) | copy-start | bytes 393220
  94.0 360.3 %copy-start.5 = (f32[128]{0:T(128)S(1)}, f32[128]{0:T(128)}, u32[]{:S(2)}) copy-start(f32[128]{0:T(128)} %param.14) | copy-start | bytes 1540
  94.0 455.2 %copy-start.3 = (f32[768]{0:T(1024)S(1)}, f32[768]{0:T(1024)}, u32[]{:S(2)}) copy-start(f32[768]{0:T(1024)} %param.16) | copy-start | bytes 9220
  94.0 283.1 %all-gather.8.cloned.1.call-start = ((), (), s32[]{:S(2)}) async-start(), calls=%async_computation.3 | async-start | bytes 1597440 | tf_op jit(solution)/shard_map/all_gather | solution.py:48
  294.4 128.6 %reduce-scatter.3.cloned.1.call-start = ((), (), s32[]{:S(2)}) async-start(), calls=%async_computation.4 | async-start | bytes 1179648 | tf_op jit(solution)/shard_map/reduce_scatter | solution.py:53
  381.4 125.0 %all-gather.12.cloned.1.call-start = ((), (), s32[]{:S(2)}) async-start(), calls=%async_computation.6 | async-start | bytes 3194880 | tf_op jit(solution)/shard_map/all_gather | solution.py:61
  382.0 167.3 %all-gather.10.cloned.1.call-start = ((), (), s32[]{:S(2)}) async-start(), calls=%async_computation.5 | async-start | bytes 1179648 | tf_op jit(solution)/shard_map/all_gather | solution.py:59
  455.1 177.6 %all-gather.14.cloned.1.call-start = ((), (), s32[]{:S(2)}) async-start(), calls=%async_computation.7 | async-start | bytes 3194880 | tf_op jit(solution)/shard_map/all_gather | solution.py:63
  455.9 225.7 %reduce-scatter.5.cloned.1.call-start = ((), (), s32[]{:S(2)}) async-start(), calls=%async_computation.8 | async-start | bytes 1179648 | tf_op jit(solution)/shard_map/reduce_scatter | solution.py:64
Sparse Core Ops, SparseCore 0:
  47.9 40.2 all-gather.5
  94.1 198.7 all-reduce.2
  296.3 80.7 all-gather.7
  381.5 41.4 reduce-scatter.2
  426.2 80.0 all-gather.11
  508.3 40.9 all-gather.9
  552.6 80.0 all-gather.13
  640.1 41.4 reduce-scatter.4
where the time goes:
time: 691 us; the launch traced here: 690 us
  waiting for transfers between devices  575 us (83%)
  blocking collectives  67.7 us (10%)
  matrix products  22.3 us (3%)
  between operations  14.2 us (2%)
  other arithmetic  7.95 us (1%)
    unnamed x9, waiting for transfers between devices  198 us
    all_gather x1, waiting for transfers between devices, shards(): lax.all_gather(activated, 'tok', axis=0, tiled=True)  82.7 us
    all_gather x1, waiting for transfers between devices, shards(): lax.all_gather(ch_out_weight, 'tok', axis=1, tiled=True)  78.4 us
    all_gather x1, waiting for transfers between devices, shards(): lax.all_gather(ch_in_weight, 'tok', axis=0, tiled=True)  50.2 us
    all_gather x1, waiting for transfers between devices, shards(): normed_two = lax.all_gather(normed_part_two, 'ch', axis=1, tiled=True)  42.9 us
    reduce_scatter x1, waiting for transfers between devices, shards(): lax.psum_scatter(channel_terms, 'ch', scatter_dimension=1, tiled=True)  41.6 us
    reduce_scatter x1, waiting for transfers between devices, shards(): lax.psum_scatter(partial_value, 'ch', scatter_dimension=1, tiled=True)  40.9 us
    all_gather x1, waiting for transfers between devices, shards(): normed = lax.all_gather(normed_part, 'ch', axis=1, tiled=True)  40.3 us
  transfers between devices with their start and end apart: 8, of which 8 were waited for; matrix products, arithmetic and copies ran while one was open for 1% of the time, Pallas kernels for 0%

commit v1 on v0

--- a/solution.py
+++ b/solution.py
@@ -5,6 +5,13 @@
 
 epsilon = 1e-05
 highest = lax.Precision.HIGHEST
+
+
+def exchange_gather(shard, name, dim):
+    count = lax.axis_size(name)
+    blocks = jnp.stack([shard for _ in range(count)])
+    blocks = lax.all_to_all(blocks, name, split_axis=0, concat_axis=0)
+    return jnp.concatenate(blocks, axis=dim)
 
 
 def matmul(left, right):
@@ -45,7 +52,7 @@
     activated = jax.nn.gelu(summed_cols + tok_in_bias[None, :], approximate=False)
     partial_value = lax.dot_general(
         tok_out_weight,
-        lax.all_gather(activated, "tok", axis=0, tiled=True),
+        exchange_gather(activated, "tok", 0),
         (((1,), (1,)), ((), ())),
         precision=highest,
         preferred_element_type=jnp.float32,

time: 691 us -> 652 us (0.944)
  waiting for transfers between devices: 575 us -> 490 us
  blocking collectives: 67.7 us -> 116 us
    all_gather x1 -> x0, waiting for transfers between devices: 82.7 us -> none  [shards(): lax.all_gather(activated, 'tok', axis=0, tiled=True)]
    all_to_all x0 -> x1, blocking collectives: none -> 48.4 us  [exchange_gather(): blocks = lax.all_to_all(blocks, name, split_axis=0, concat_axis=0)]
    unnamed x9 -> x8, waiting for transfers between devices: 198 us -> 198 us
  transfers between devices with their start and end apart: 8 -> 7, of which waited for: 8 -> 7; matrix products, arithmetic and copies ran while one was open for 1% -> 1% of each run, Pallas kernels for 0% -> 0%
where the time goes in v1:
time: 652 us; the launch traced here: 651 us
  waiting for transfers between devices  490 us (75%)
  blocking collectives  116 us (18%)
  matrix products  20.9 us (3%)
  between operations  14.2 us (2%)
  other arithmetic  7.32 us (1%)
    unnamed x8, waiting for transfers between devices  198 us
    all_gather x1, waiting for transfers between devices, shards(): lax.all_gather(ch_out_weight, 'tok', axis=1, tiled=True)  78.3 us
    all_gather x1, waiting for transfers between devices, shards(): lax.all_gather(ch_in_weight, 'tok', axis=0, tiled=True)  50.4 us
    all_to_all x1, blocking collectives, exchange_gather(): blocks = lax.all_to_all(blocks, name, split_axis=0, concat_axis=0)  48.4 us
    all_gather x1, waiting for transfers between devices, shards(): normed_two = lax.all_gather(normed_part_two, 'ch', axis=1, tiled=True)  42.9 us
    reduce_scatter x1, waiting for transfers between devices, shards(): lax.psum_scatter(channel_terms, 'ch', scatter_dimension=1, tiled=True)  41.7 us
    all_gather x1, waiting for transfers between devices, shards(): normed = lax.all_gather(normed_part, 'ch', axis=1, tiled=True)  40.3 us
    reduce_scatter x1, waiting for transfers between devices, shards(): lax.psum_scatter(partial_value, 'ch', scatter_dimension=1, tiled=True)  38.4 us
  transfers between devices with their start and end apart: 7, of which 7 were waited for; matrix products, arithmetic and copies ran while one was open for 1% of the time, Pallas kernels for 0%

profile of v1, /device:TPU:2, one launch (start us, length us, event | category | flops | bytes accessed | tf_op | source)
XLA Modules:
  0.0 651.3 jit_solution(15267602252553994532)
XLA Ops:
  6.5 0.0 copy-start
  6.5 0.0 all-gather.5.cloned.1.call-start
  6.5 1.1 reduce_sum.36
  7.6 23.2 %psum.28 = f32[256,1]{0,1:T(1,128)S(1)} all-reduce(f32[256,1]{0,1:T(1,128)S(1)} %bitcast.27), channel_id=1, replica_groups=mesh['tok'=64,'ch'=8] {'ch'}, use_global_device_ids=true, to_apply=%region_1.0 | all-reduce | flops 256 | bytes 2048 | tf_op jit(solution)/shard_map/psum | solution.py:34
  30.8 1.1 multiply_reduce_fusion.1
  31.9 14.2 %psum.29 = f32[256,1]{0,1:T(1,128)S(1)} all-reduce(f32[256,1]{0,1:T(1,128)S(1)} %bitcast.28), channel_id=1, replica_groups=mesh['tok'=64,'ch'=8] {'ch'}, use_global_device_ids=true, to_apply=%region_3.0 | all-reduce | flops 256 | bytes 2048 | tf_op jit(solution)/shard_map/psum | solution.py:36
  46.1 1.7 multiply_multiply_fusion.6
  47.8 0.0 all-gather.5.cloned.1.call-update
  47.8 0.0 copy-start.4
  47.8 0.0 all-reduce.3.cloned.1.call-start
  47.8 40.3 %all-gather.5.cloned.1.call-done = f32[256,1024]{1,0:T(8,128)} async-done(((f32[256,128]{1,0:T(8,128)}), f32[256,1024]{1,0:T(8,128)}) %all-gather.5.cloned.1.call-update) | async-done | bytes 1048592 | tf_op jit(solution)/shard_map/all_gather | solution.py:38
  88.2 0.0 copy-done
  88.2 5.8 fusion.129
  94.0 0.0 all-reduce.3.cloned.1.call-update
  94.0 0.0 reduce-scatter.3.cloned.1.call-start
  94.0 1.3 dynamic-slice
  96.0 197.0 %all-reduce.3.cloned.1.call-done = f32[1024,384]{1,0:T(8,128)} async-done(((f32[1024,384]{1,0:T(8,128)}), f32[1024,384]{1,0:T(8,128)}) %all-reduce.3.cloned.1.call-update) | async-done | bytes 1572880
  292.9 0.0 copy-done.4
  292.9 0.8 fusion.90
  293.7 0.1 stack.2
  293.9 0.0 copy-start.2
  293.9 48.4 %all_to_all.5 = f32[64,16,384]{2,1,0:T(8,128)S(1)} all-to-all(f32[64,16,384]{2,1,0:T(8,128)S(1)} %stack.2), channel_id=1, replica_groups=mesh['tok'=64,'ch'=8] {'tok'}, dimensions={0} | all-to-all | bytes 3145728 | tf_op jit(solution)/shard_map/all_to_all | solution.py:13
  342.3 0.0 copy-done.2
  342.3 0.0 copy-start.1
  342.3 2.8 convolution_bitcast_fusion
  345.1 0.0 copy-start.5
  345.1 0.0 copy-start.3
  345.1 0.0 reduce-scatter.3.cloned.1.call-update
  345.1 0.0 all-gather.9.cloned.1.call-start
  345.2 0.5 all-gather.9.cloned.1.call-update
  345.7 0.0 all-gather.7.cloned.1.call-start
  345.7 0.0 copy-done.1
  345.8 0.1 copy.16
  345.9 38.4 %reduce-scatter.3.cloned.1.call-done = f32[256,128]{0,1:T(8,128)} async-done(((f32[256,1024]{0,1:T(8,128)}), f32[256,128]{0,1:T(8,128)}) %reduce-scatter.3.cloned.1.call-update) | async-done | bytes 131088 | tf_op jit(solution)/shard_map/reduce_scatter | solution.py:60
  384.2 0.9 fusion.128
  385.2 15.4 %psum.30 = f32[256,1]{0,1:T(1,128)S(1)} all-reduce(f32[256,1]{0,1:T(1,128)S(1)} %bitcast.24), channel_id=1, replica_groups=mesh['tok'=64,'ch'=8] {'ch'}, use_global_device_ids=true, to_apply=%region_7.0 | all-reduce | flops 256 | bytes 2048 | tf_op jit(solution)/shard_map/psum | solution.py:62
  400.7 14.9 %psum.31 = f32[256,1]{0,1:T(1,128)S(1)} all-reduce(f32[256,1]{0,1:T(1,128)S(1)} %bitcast.29), channel_id=1, replica_groups=mesh['tok'=64,'ch'=8] {'ch'}, use_global_device_ids=true, to_apply=%region_9.0 | all-reduce | flops 256 | bytes 2048 | tf_op jit(solution)/shard_map/psum | solution.py:64
  415.5 0.0 copy-done.5
  415.5 0.7 multiply_multiply_fusion.5
  416.3 0.0 all-gather.7.cloned.1.call-update
  416.3 0.0 all-gather.11.cloned.1.call-start
  416.4 0.5 all-gather.11.cloned.1.call-update
  416.9 0.2 reduce-scatter.5.cloned.1.call-start
  417.1 50.4 %all-gather.9.cloned.1.call-done = f32[1024,768]{1,0:T(8,128)} async-done(((f32[16,768]{1,0:T(8,128)}), f32[1024,768]{1,0:T(8,128)}) %all-gather.9.cloned.1.call-update) | async-done | bytes 3145744 | tf_op jit(solution)/shard_map/all_gather | solution.py:68
  467.5 42.9 %all-gather.7.cloned.1.call-done = f32[256,1024]{0,1:T(8,128)} async-done(((f32[256,128]{0,1:T(8,128)}), f32[256,1024]{0,1:T(8,128)}) %all-gather.7.cloned.1.call-update) | async-done | bytes 1048592 | tf_op jit(solution)/shard_map/all_gather | solution.py:66
  510.4 0.0 copy-done.3
  510.4 5.0 convolution_add_fusion
  515.4 78.3 %all-gather.11.cloned.1.call-done = f32[768,1024]{0,1:T(8,128)} async-done(((f32[768,16]{0,1:T(8,128)}), f32[768,1024]{0,1:T(8,128)}) %all-gather.11.cloned.1.call-update) | async-done | bytes 3145744 | tf_op jit(solution)/shard_map/all_gather | solution.py:70
  593.7 7.3 %fusion.2 = f32[256,1024]{0,1:T(8,128)} fusion(f32[768,1024]{0,1:T(8,128)} %all-gather.11.cloned.1.call-done, f32[256,768]{1,0:T(8,128)S(1)} %convolution_add_fusion), kind=kOutput, calls=%fused_computation.5 | convolution fusion | flops 2428502016 | bytes 4980736 | tf_op jit(solution)/shard_map/dot_general | solution.py:18
  601.0 0.0 reduce-scatter.5.cloned.1.call-update
  601.0 41.7 %reduce-scatter.5.cloned.1.call-done = f32[256,128]{0,1:T(8,128)} async-done(((f32[256,1024]{0,1:T(8,128)}), f32[256,128]{0,1:T(8,128)}) %reduce-scatter.5.cloned.1.call-update) | async-done | bytes 131088 | tf_op jit(solution)/shard_map/reduce_scatter | solution.py:71
  642.8 0.9 add.49
  643.7 0.8 copy.18
  (5 shorter events, 0.1 us)
Async XLA Ops:
  6.5 81.6 %copy-start = (f32[384,256]{1,0:T(8,128)S(1)}, f32[384,256]{1,0:T(8,128)}, u32[]{:S(2)}) copy-start(f32[384,256]{1,0:T(8,128)} %param.11) | copy-start | bytes 1179652
  6.5 81.6 %all-gather.5.cloned.1.call-start = ((), (), s32[]{:S(2)}) async-start(), calls=%async_computation.3 | async-start | bytes 1179648 | tf_op jit(solution)/shard_map/all_gather | solution.py:38
  47.8 245.2 %copy-start.4 = (f32[384]{0:T(512)S(1)}, f32[384]{0:T(512)}, u32[]{:S(2)}) copy-start(f32[384]{0:T(512)} %param.12) | copy-start | bytes 4612
  47.8 245.1 %all-reduce.3.cloned.1.call-start = ((), (), s32[]{:S(2)}) async-start(), calls=%async_computation.9 | async-start | bytes 3145728
  94.0 290.2 %reduce-scatter.3.cloned.1.call-start = ((), (), s32[]{:S(2)}) async-start(), calls=%async_computation.4 | async-start | bytes 1179648 | tf_op jit(solution)/shard_map/reduce_scatter | solution.py:60
  293.9 48.4 %copy-start.2 = (f32[256,384]{1,0:T(8,128)S(1)}, f32[256,384]{1,0:T(8,128)}, u32[]{:S(2)}) copy-start(f32[256,384]{1,0:T(8,128)} %param.13) | copy-start | bytes 1179652
  342.3 3.4 copy-start.1
  345.1 70.5 %copy-start.5 = (f32[128]{0:T(128)S(1)}, f32[128]{0:T(128)}, u32[]{:S(2)}) copy-start(f32[128]{0:T(128)} %param.14) | copy-start | bytes 1540
  345.1 165.3 %copy-start.3 = (f32[768]{0:T(1024)S(1)}, f32[768]{0:T(1024)}, u32[]{:S(2)}) copy-start(f32[768]{0:T(1024)} %param.16) | copy-start | bytes 9220
  345.1 122.4 %all-gather.9.cloned.1.call-start = ((), (), s32[]{:S(2)}) async-start(), calls=%async_computation.6 | async-start | bytes 3194880 | tf_op jit(solution)/shard_map/all_gather | solution.py:68
  345.7 164.7 %all-gather.7.cloned.1.call-start = ((), (), s32[]{:S(2)}) async-start(), calls=%async_computation.5 | async-start | bytes 1179648 | tf_op jit(solution)/shard_map/all_gather | solution.py:66
  416.3 177.4 %all-gather.11.cloned.1.call-start = ((), (), s32[]{:S(2)}) async-start(), calls=%async_computation.7 | async-start | bytes 3194880 | tf_op jit(solution)/shard_map/all_gather | solution.py:70
  416.9 225.9 %reduce-scatter.5.cloned.1.call-start = ((), (), s32[]{:S(2)}) async-start(), calls=%async_computation.8 | async-start | bytes 1179648 | tf_op jit(solution)/shard_map/reduce_scatter | solution.py:71
Sparse Core Ops, SparseCore 0:
  47.9 40.2 all-gather.4
  94.1 198.7 all-reduce.2
  345.2 38.9 reduce-scatter.2
  387.4 80.0 all-gather.8
  469.4 40.9 all-gather.6
  513.6 80.0 all-gather.10
  601.1 41.5 reduce-scatter.4
